TPU v7x, 32 devices: a whole 2x2x4 slice. The times are simulated.
32 devices in a mesh: rows: 8 (over z, y), grp: 4 (over x, core).
Axes of the slice: x: 2, y: 2, z: 4, core: 2. Of those that a mesh axis runs over, the one named last changes fastest.
Arguments:
- rhs: float32 [3, 8, 4, 2, 512], P(None, 'rows', 'grp'), may hold values from -6 to 6
- diag_inverse: bfloat16 [3, 8, 4, 512, 512], P(None, 'rows', 'grp'), as said below
- coupling: bfloat16 [3, 8, 4, 512, 512], P(None, 'rows', 'grp'), may hold values from -0.125 to 0.125
- off_block: bfloat16 [2, 8, 4, 512, 512], P(None, 'rows', 'grp'), may hold values from -0.1875 to 0.1875
- off_route: int32 [2, 8, 4], P(None, 'rows', 'grp'), may hold values from 0 to 15, as said below
Outputs:
- solution: float32 [3, 8, 4, 2, 512], P(None, 'rows', 'grp')
Inputs may be any that keep to these rules, and one draw needn't show every extreme that they name: `off_route`: for a block of super-level l the value is s * 8 + t with 0 <= s <= 1 - l: the block belongs to block row t of the same group in super-level l + 1 + s. `diag_inverse`: each matrix is a dominant diagonal plus independent off-diagonal entries.
All inputs are finite; a program needn't handle non-finite values.
Results may differ from a plain program's by a relative error of at most 0.0045.
Values may be sent and summed in bfloat16 or wider, within the bound.
No kernel may reach another device: no remote copies, remote signals or barrier semaphores. Data moves between devices by JAX's collectives and lax.ppermute only.
A program may use at most 64 MiB of HBM per device.

v0:
```python
import jax
import jax.numpy as jnp
from jax import lax
from jax.sharding import PartitionSpec as P


def shifted(value, axis, steps):
    count = lax.axis_size(axis)
    first, last = (max(0, -steps), min(count, count - steps))
    return lax.ppermute(value, axis, [(source, source + steps) for source in range(first, last)])


def shards(rhs, diag_inverse, coupling, off_block, off_route):
    highest = lax.Precision.HIGHEST
    levels = rhs.shape[0]
    groups = lax.axis_size("grp")
    rowblocks = lax.axis_size("rows")
    source_all = rhs[:, 0, 0]
    inverse_all = diag_inverse[:, 0, 0]
    coupler_all = coupling[:, 0, 0]
    blocks = off_block[:, 0, 0]
    routes = off_route[:, 0, 0]
    pending = [jnp.zeros(source_all.shape[1:], jnp.float32) for index_value in range(levels)]
    results = []
    for super_level in range(levels):
        source = source_all[super_level] - pending[super_level]
        inverse = inverse_all[super_level].astype(jnp.float32)
        coupler = coupler_all[super_level].astype(jnp.float32)
        solved = jnp.dot(source, inverse, precision=highest)
        for repeat in range(groups - 1):
            before = shifted(solved, "grp", 1)
            solved = jnp.dot(
                source - jnp.dot(before, coupler, precision=highest), inverse, precision=highest
            )
        results.append(solved)
        if super_level < levels - 1:
            contribution = jnp.dot(
                solved.astype(jnp.bfloat16), blocks[super_level], preferred_element_type=jnp.float32
            ).astype(jnp.bfloat16)
            ahead_count = levels - 1 - super_level
            routing = routes[super_level]
            level_skip = routing // rowblocks
            target_row = routing % rowblocks
            one_hot = (jnp.arange(ahead_count, dtype=jnp.int32)[:, None] == level_skip) & (
                jnp.arange(rowblocks, dtype=jnp.int32)[None, :] == target_row
            )
            send_buffer = jnp.where(
                one_hot[:, :, None, None], contribution[None, None], jnp.zeros((), jnp.bfloat16)
            )
            received = lax.all_to_all(send_buffer, "rows", split_axis=1, concat_axis=1, tiled=True)
            arrived = jnp.sum(received.astype(jnp.float32), axis=1)
            for ahead in range(ahead_count):
                pending[super_level + 1 + ahead] = pending[super_level + 1 + ahead] + arrived[ahead]
    return jnp.stack(results, axis=0)[:, None, None]


def solution(mesh):
    return jax.shard_map(
        shards,
        mesh=mesh,
        in_specs=(
            P(None, "rows", "grp", None, None),
            P(None, "rows", "grp", None, None),
            P(None, "rows", "grp", None, None),
            P(None, "rows", "grp", None, None),
            P(None, "rows", "grp"),
        ),
        out_specs=P(None, "rows", "grp", None, None),
        check_vma=False,
    )
```

profile of v0, /device:TPU:1, one launch (start us, length us, event | category | flops | bytes accessed | tf_op | source)
XLA Modules:
  0.0 80.2 jit_solution(13542884411301411389)
XLA Ops:
  0.0 1.5 %fusion.32 = f32[2,512]{1,0:T(2,128)S(1)} fusion(bf16[3,1,1,512,512]{4,3,2,1,0:T(8,128)(2,1)} %param.6, f32[3,1,1,2,512]{4,3,2,1,0:T(2,128)} %param.5), kind=kOutput, calls=%fused_computation.44 | convolution fusion | flops 6291456 | bytes 532480 | tf_op jit(solution)/shard_map/dot_general | solution.py:29
  1.5 4.5 %collective-permute-start = (f32[2,512]{1,0:T(2,128)S(1)}, f32[2,512]{1,0:T(2,128)S(1)}, u32[]{:S(2)}, u32[]{:S(2)}) collective-permute-start(f32[2,512]{1,0:T(2,128)S(1)} %fusion.32), channel_id=1, source_target_pairs={{0,1},{1,2},{2,3},{4,5},{5,6},{6,7},{8,9},{9,10},{10,11},{12,13},{... | collective-permute-start | bytes 12296 | tf_op jit(solution)/shard_map/ppermute | solution.py:10
  6.0 1.4 %fusion.71 = (s32[1,1,1]{0,2,1:T(1,128)}, s32[1,1,1]{0,2,1:T(1,128)}) fusion(s32[2,1,1]{0,2,1:T(1,128)} %param.9), kind=kLoop, calls=%fused_computation.95 | loop fusion | bytes 16 | tf_op jit(solution)/shard_map/slice | solution.py:41
  10.0 1.4 %convolution_subtract_fusion.8 = f32[2,512]{1,0:T(2,128)S(1)} fusion(f32[2,512]{1,0:T(2,128)S(1)} %collective-permute-done, bf16[3,1,1,512,512]{4,3,2,1,0:T(8,128)(2,1)} %param.7, f32[3,1,1,2,512]{4,3,2,1,0:T(2,128)} %param.5), kind=kOutput, calls=%fused_computation.9 | convolution fusion | flops 6292480 | bytes 536576 | tf_op jit(solution)/shard_map/dot_general | solution.py:33
  11.5 1.4 %fusion.30 = f32[2,512]{1,0:T(2,128)S(1)} fusion(f32[2,512]{1,0:T(2,128)S(1)} %convolution_subtract_fusion.8, bf16[3,1,1,512,512]{4,3,2,1,0:T(8,128)(2,1)} %param.6), kind=kOutput, calls=%fused_computation.42 | convolution fusion | flops 6291456 | bytes 532480 | tf_op jit(solution)/shard_map/dot_general | solution.py:32
  12.8 1.9 %collective-permute-start.1 = (f32[2,512]{1,0:T(2,128)S(1)}, f32[2,512]{1,0:T(2,128)S(1)}, u32[]{:S(2)}, u32[]{:S(2)}) collective-permute-start(f32[2,512]{1,0:T(2,128)S(1)} %fusion.30), channel_id=1, source_target_pairs={{0,1},{1,2},{2,3},{4,5},{5,6},{6,7},{8,9},{9,10},{10,11},{12,13},{... | collective-permute-start | bytes 12296 | tf_op jit(solution)/shard_map/ppermute | solution.py:10
  14.8 1.1 %collective-permute-done.1 = f32[2,512]{1,0:T(2,128)S(1)} collective-permute-done((f32[2,512]{1,0:T(2,128)S(1)}, f32[2,512]{1,0:T(2,128)S(1)}, u32[]{:S(2)}, u32[]{:S(2)}) %collective-permute-start.1) | collective-permute-done | bytes 4128 | tf_op jit(solution)/shard_map/ppermute | solution.py:10
  15.9 1.3 %convolution_subtract_fusion.7 = f32[2,512]{1,0:T(2,128)S(1)} fusion(f32[2,512]{1,0:T(2,128)S(1)} %collective-permute-done.1, bf16[3,1,1,512,512]{4,3,2,1,0:T(8,128)(2,1)} %param.7, f32[3,1,1,2,512]{4,3,2,1,0:T(2,128)S(1)} %copy-done.4), kind=kOutput, calls=%fused_computation.8 | convolution fusion | flops 6292480 | bytes 536576 | tf_op jit(solution)/shard_map/dot_general | solution.py:33
  17.2 0.3 fusion.28
  17.6 3.8 %collective-permute-start.2 = (f32[2,512]{1,0:T(2,128)S(1)}, f32[2,512]{1,0:T(2,128)S(1)}, u32[]{:S(2)}, u32[]{:S(2)}) collective-permute-start(f32[2,512]{1,0:T(2,128)S(1)} %fusion.28), channel_id=1, source_target_pairs={{0,1},{1,2},{2,3},{4,5},{5,6},{6,7},{8,9},{9,10},{10,11},{12,13},{... | collective-permute-start | bytes 12296 | tf_op jit(solution)/shard_map/ppermute | solution.py:10
  21.4 0.7 collective-permute-done.2
  22.1 1.3 %convolution_subtract_fusion.6 = f32[2,512]{1,0:T(2,128)S(1)} fusion(f32[2,512]{1,0:T(2,128)S(1)} %collective-permute-done.2, bf16[3,1,1,512,512]{4,3,2,1,0:T(8,128)(2,1)} %param.7, f32[3,1,1,2,512]{4,3,2,1,0:T(2,128)S(1)} %copy-done.4), kind=kOutput, calls=%fused_computation.7 | convolution fusion | flops 6292480 | bytes 536576 | tf_op jit(solution)/shard_map/dot_general | solution.py:33
  23.4 0.3 fusion.26
  24.1 10.9 %all_to_all.10 = bf16[2,8,2,512]{3,2,0,1:T(2,128)(2,1)S(1)} all-to-all(bf16[2,8,2,512]{3,2,0,1:T(2,128)(2,1)S(1)} %broadcast_select_fusion), channel_id=1, replica_groups=mesh['rows'=8,'grp'=4] {'rows'}, dimensions={1} | all-to-all | bytes 65536 | tf_op jit(solution)/shard_map/all_to_all | solution.py:50
  35.3 5.6 %collective-permute-start.3 = (f32[2,512]{1,0:T(2,128)S(1)}, f32[2,512]{1,0:T(2,128)S(1)}, u32[]{:S(2)}, u32[]{:S(2)}) collective-permute-start(f32[2,512]{1,0:T(2,128)S(1)} %fusion.20), channel_id=1, source_target_pairs={{0,1},{1,2},{2,3},{4,5},{5,6},{6,7},{8,9},{9,10},{10,11},{12,13},{... | collective-permute-start | bytes 12296 | tf_op jit(solution)/shard_map/ppermute | solution.py:10
  40.9 0.7 collective-permute-done.3
  42.0 0.3 fusion.18
  42.3 4.2 %collective-permute-start.4 = (f32[2,512]{1,0:T(2,128)S(1)}, f32[2,512]{1,0:T(2,128)S(1)}, u32[]{:S(2)}, u32[]{:S(2)}) collective-permute-start(f32[2,512]{1,0:T(2,128)S(1)} %fusion.18), channel_id=1, source_target_pairs={{0,1},{1,2},{2,3},{4,5},{5,6},{6,7},{8,9},{9,10},{10,11},{12,13},{... | collective-permute-start | bytes 12296 | tf_op jit(solution)/shard_map/ppermute | solution.py:10
  49.3 0.3 fusion.16
  49.7 2.4 %collective-permute-start.5 = (f32[2,512]{1,0:T(2,128)S(1)}, f32[2,512]{1,0:T(2,128)S(1)}, u32[]{:S(2)}, u32[]{:S(2)}) collective-permute-start(f32[2,512]{1,0:T(2,128)S(1)} %fusion.16), channel_id=1, source_target_pairs={{0,1},{1,2},{2,3},{4,5},{5,6},{6,7},{8,9},{9,10},{10,11},{12,13},{... | collective-permute-start | bytes 12296 | tf_op jit(solution)/shard_map/ppermute | solution.py:10
  52.0 0.7 collective-permute-done.5
  53.7 7.8 %all_to_all.11 = bf16[1,8,2,512]{3,2,0,1:T(2,128)(2,1)S(1)} all-to-all(bf16[1,8,2,512]{3,2,0,1:T(2,128)(2,1)S(1)} %broadcast_select_fusion.1), channel_id=1, replica_groups=mesh['rows'=8,'grp'=4] {'rows'}, dimensions={1} | all-to-all | bytes 32768 | tf_op jit(solution)/shard_map/all_to_all | solution.py:50
  61.8 5.3 %collective-permute-start.6 = (f32[2,512]{1,0:T(2,128)S(1)}, f32[2,512]{1,0:T(2,128)S(1)}, u32[]{:S(2)}, u32[]{:S(2)}) collective-permute-start(f32[2,512]{1,0:T(2,128)S(1)} %fusion.8), channel_id=1, source_target_pairs={{0,1},{1,2},{2,3},{4,5},{5,6},{6,7},{8,9},{9,10},{10,11},{12,13},{... | collective-permute-start | bytes 12296 | tf_op jit(solution)/shard_map/ppermute | solution.py:10
  67.2 0.7 collective-permute-done.6
  68.2 0.3 fusion.6
  68.5 4.2 %collective-permute-start.7 = (f32[2,512]{1,0:T(2,128)S(1)}, f32[2,512]{1,0:T(2,128)S(1)}, u32[]{:S(2)}, u32[]{:S(2)}) collective-permute-start(f32[2,512]{1,0:T(2,128)S(1)} %fusion.6), channel_id=1, source_target_pairs={{0,1},{1,2},{2,3},{4,5},{5,6},{6,7},{8,9},{9,10},{10,11},{12,13},{... | collective-permute-start | bytes 12296 | tf_op jit(solution)/shard_map/ppermute | solution.py:10
  72.7 0.7 collective-permute-done.7
  73.7 0.3 fusion.4
  74.1 4.2 %collective-permute-start.8 = (f32[2,512]{1,0:T(2,128)S(1)}, f32[2,512]{1,0:T(2,128)S(1)}, u32[]{:S(2)}, u32[]{:S(2)}) collective-permute-start(f32[2,512]{1,0:T(2,128)S(1)} %fusion.4), channel_id=1, source_target_pairs={{0,1},{1,2},{2,3},{4,5},{5,6},{6,7},{8,9},{9,10},{10,11},{12,13},{... | collective-permute-start | bytes 12296 | tf_op jit(solution)/shard_map/ppermute | solution.py:10
  78.3 0.7 collective-permute-done.8
  79.3 0.3 convolution_bitcast_fusion
  79.6 0.6 maximum_bitcast_fusion
  (32 shorter events, 3.5 us)
Async XLA Ops:
  0.0 17.2 %copy-start = (bf16[3,1,1,512,512]{4,3,2,1,0:T(8,128)(2,1)S(1)}, bf16[3,1,1,512,512]{4,3,2,1,0:T(8,128)(2,1)}, u32[]{:S(2)}) copy-start(bf16[3,1,1,512,512]{4,3,2,1,0:T(8,128)(2,1)} %param.6) | copy-start | bytes 4718596
  0.0 15.9 %copy-start.4 = (f32[3,1,1,2,512]{4,3,2,1,0:T(2,128)S(1)}, f32[3,1,1,2,512]{4,3,2,1,0:T(2,128)}, u32[]{:S(2)}) copy-start(f32[3,1,1,2,512]{4,3,2,1,0:T(2,128)} %param.5) | copy-start | bytes 36868
  1.5 8.5 %collective-permute-start = (f32[2,512]{1,0:T(2,128)S(1)}, f32[2,512]{1,0:T(2,128)S(1)}, u32[]{:S(2)}, u32[]{:S(2)}) collective-permute-start(f32[2,512]{1,0:T(2,128)S(1)} %fusion.32), channel_id=1, source_target_pairs={{0,1},{1,2},{2,3},{4,5},{5,6},{6,7},{8,9},{9,10},{10,11},{12,13},{... | collective-permute-start | bytes 12296 | tf_op jit(solution)/shard_map/ppermute | solution.py:10
  10.0 13.8 %copy-start.2 = (bf16[2,1,1,512,512]{4,3,2,1,0:T(8,128)(2,1)S(1)}, bf16[2,1,1,512,512]{4,3,2,1,0:T(8,128)(2,1)}, u32[]{:S(2)}) copy-start(bf16[2,1,1,512,512]{4,3,2,1,0:T(8,128)(2,1)} %param.8) | copy-start | bytes 3145732
  12.8 3.1 %collective-permute-start.1 = (f32[2,512]{1,0:T(2,128)S(1)}, f32[2,512]{1,0:T(2,128)S(1)}, u32[]{:S(2)}, u32[]{:S(2)}) collective-permute-start(f32[2,512]{1,0:T(2,128)S(1)} %fusion.30), channel_id=1, source_target_pairs={{0,1},{1,2},{2,3},{4,5},{5,6},{6,7},{8,9},{9,10},{10,11},{12,13},{... | collective-permute-start | bytes 12296 | tf_op jit(solution)/shard_map/ppermute | solution.py:10
  14.8 26.9 %copy-start.1 = (bf16[3,1,1,512,512]{4,3,2,1,0:T(8,128)(2,1)S(1)}, bf16[3,1,1,512,512]{4,3,2,1,0:T(8,128)(2,1)}, u32[]{:S(2)}) copy-start(bf16[3,1,1,512,512]{4,3,2,1,0:T(8,128)(2,1)} %param.7) | copy-start | bytes 4718596
  17.6 4.5 %collective-permute-start.2 = (f32[2,512]{1,0:T(2,128)S(1)}, f32[2,512]{1,0:T(2,128)S(1)}, u32[]{:S(2)}, u32[]{:S(2)}) collective-permute-start(f32[2,512]{1,0:T(2,128)S(1)} %fusion.28), channel_id=1, source_target_pairs={{0,1},{1,2},{2,3},{4,5},{5,6},{6,7},{8,9},{9,10},{10,11},{12,13},{... | collective-permute-start | bytes 12296 | tf_op jit(solution)/shard_map/ppermute | solution.py:10
  35.3 6.4 %collective-permute-start.3 = (f32[2,512]{1,0:T(2,128)S(1)}, f32[2,512]{1,0:T(2,128)S(1)}, u32[]{:S(2)}, u32[]{:S(2)}) collective-permute-start(f32[2,512]{1,0:T(2,128)S(1)} %fusion.20), channel_id=1, source_target_pairs={{0,1},{1,2},{2,3},{4,5},{5,6},{6,7},{8,9},{9,10},{10,11},{12,13},{... | collective-permute-start | bytes 12296 | tf_op jit(solution)/shard_map/ppermute | solution.py:10
  42.3 6.7 %collective-permute-start.4 = (f32[2,512]{1,0:T(2,128)S(1)}, f32[2,512]{1,0:T(2,128)S(1)}, u32[]{:S(2)}, u32[]{:S(2)}) collective-permute-start(f32[2,512]{1,0:T(2,128)S(1)} %fusion.18), channel_id=1, source_target_pairs={{0,1},{1,2},{2,3},{4,5},{5,6},{6,7},{8,9},{9,10},{10,11},{12,13},{... | collective-permute-start | bytes 12296 | tf_op jit(solution)/shard_map/ppermute | solution.py:10
  49.0 4.4 %copy-start.3 = (bf16[2,1,1,512,512]{4,3,2,1,0:T(8,128)(2,1)S(1)}, bf16[2,1,1,512,512]{4,3,2,1,0:T(8,128)(2,1)}, u32[]{:S(2)}) copy-start(bf16[2,1,1,512,512]{4,3,2,1,0:T(8,128)(2,1)} %param.8) | copy-start | bytes 3145732
  49.7 3.1 %collective-permute-start.5 = (f32[2,512]{1,0:T(2,128)S(1)}, f32[2,512]{1,0:T(2,128)S(1)}, u32[]{:S(2)}, u32[]{:S(2)}) collective-permute-start(f32[2,512]{1,0:T(2,128)S(1)} %fusion.16), channel_id=1, source_target_pairs={{0,1},{1,2},{2,3},{4,5},{5,6},{6,7},{8,9},{9,10},{10,11},{12,13},{... | collective-permute-start | bytes 12296 | tf_op jit(solution)/shard_map/ppermute | solution.py:10
  61.8 6.1 %collective-permute-start.6 = (f32[2,512]{1,0:T(2,128)S(1)}, f32[2,512]{1,0:T(2,128)S(1)}, u32[]{:S(2)}, u32[]{:S(2)}) collective-permute-start(f32[2,512]{1,0:T(2,128)S(1)} %fusion.8), channel_id=1, source_target_pairs={{0,1},{1,2},{2,3},{4,5},{5,6},{6,7},{8,9},{9,10},{10,11},{12,13},{... | collective-permute-start | bytes 12296 | tf_op jit(solution)/shard_map/ppermute | solution.py:10
  68.5 4.9 %collective-permute-start.7 = (f32[2,512]{1,0:T(2,128)S(1)}, f32[2,512]{1,0:T(2,128)S(1)}, u32[]{:S(2)}, u32[]{:S(2)}) collective-permute-start(f32[2,512]{1,0:T(2,128)S(1)} %fusion.6), channel_id=1, source_target_pairs={{0,1},{1,2},{2,3},{4,5},{5,6},{6,7},{8,9},{9,10},{10,11},{12,13},{... | collective-permute-start | bytes 12296 | tf_op jit(solution)/shard_map/ppermute | solution.py:10
  74.1 4.9 %collective-permute-start.8 = (f32[2,512]{1,0:T(2,128)S(1)}, f32[2,512]{1,0:T(2,128)S(1)}, u32[]{:S(2)}, u32[]{:S(2)}) collective-permute-start(f32[2,512]{1,0:T(2,128)S(1)} %fusion.4), channel_id=1, source_target_pairs={{0,1},{1,2},{2,3},{4,5},{5,6},{6,7},{8,9},{9,10},{10,11},{12,13},{... | collective-permute-start | bytes 12296 | tf_op jit(solution)/shard_map/ppermute | solution.py:10
where the time goes:
time: 80.9 us; the launch traced here: 80.2 us
  starting transfers between devices  36.1 us (45%)
  blocking collectives  18.7 us (23%)
  matrix products  12.3 us (15%)
  waiting for transfers between devices  5.4 us (7%)
  between operations  5.32 us (7%)
  local copies, waits for them, and re-layouts  1.39 us (2%)
  other arithmetic  1.01 us (1%)
    ppermute x9, starting transfers between devices, shifted(): lax.ppermute(value, axis, [(source, source + steps) for source in range(f...  36.1 us
    all_to_all x2, blocking collectives, shards(): lax.all_to_all(send_buffer, 'rows', split_axis=1, concat_axis=1, tiled=True)  18.7 us
    dot_general x9, matrix products, shards(): jnp.dot(before, coupler, precision=highest)  5.96 us
    ppermute x9, waiting for transfers between devices, shifted(): lax.ppermute(value, axis, [(source, source + steps) for source in range(f...  5.4 us
    dot_general x9, matrix products, shards(): jnp.dot(source - jnp.dot(before, coupler, precision=highest), inverse, pr...  3.9 us
    dot_general x3, matrix products, shards(): solved = jnp.dot(source, inverse, precision=highest)  2.1 us
  transfers between devices with their start and end apart: 9, of which 7 were waited for; matrix products, arithmetic and copies ran while one was open for 2% of the time, Pallas kernels for 0%

commit v1 on v0

v1 whole, which is shorter than its diff:
```python
import jax
import jax.numpy as jnp
from jax import lax
from jax.sharding import PartitionSpec as P

INNER = 2


def product(x, w):
    high = x.astype(jnp.bfloat16)
    low = (x - high.astype(jnp.float32)).astype(jnp.bfloat16)
    both = jnp.dot(jnp.concatenate([high, low], axis=0), w, preferred_element_type=jnp.float32)
    return both[: x.shape[0]] + both[x.shape[0] :]


def shards(rhs, diag_inverse, coupling, off_block, off_route):
    axes = ("rows", "grp")
    levels, nrhs, width = rhs.shape[0], rhs.shape[3], rhs.shape[4]
    groups, rowblocks = lax.axis_size("grp"), lax.axis_size("rows")
    outer = groups // INNER
    group = lax.axis_index("grp")
    chip, core = group // INNER, group % INNER
    first = core == 0
    source_all = rhs[:, 0, 0]
    inverse, coupler, blocks = diag_inverse[:, 0, 0], coupling[:, 0, 0], off_block[:, 0, 0]
    routes = off_route[:, 0, 0]

    flip = [(g, g ^ 1) for g in range(groups)]
    straight = [(g, (g + INNER) % groups) for g in range(groups)]
    cross = [(g, (g ^ 1) + INNER if (g ^ 1) + INNER < groups else (g ^ 1) + INNER - groups) for g in range(groups)]

    u = product(source_all[0], inverse[0])
    swapped = lax.ppermute(jnp.concatenate([u[None], source_all[1:]], axis=0), "grp", flip)
    inverse_p = lax.ppermute(inverse, "grp", flip)
    coupler_p = lax.ppermute(coupler, "grp", flip)

    device = jnp.arange(rowblocks * groups, dtype=jnp.int32)
    to_row, to_chip = device // groups, (device % groups) // INNER
    results, held = [], None
    incoming = [None] * levels
    for level in range(levels):
        if level == 0:
            u_own, u_other = u, swapped[0]
        else:
            own = jnp.where(first, incoming[level][0], incoming[level][1])
            other = jnp.where(first, incoming[level][1], incoming[level][0])
            u_own = product(source_all[level] - own, inverse[level])
            u_other = product(swapped[level] - other, inverse_p[level])
        z = jnp.where(first, 0.0, u_other)
        solved = u_own - product(product(z, coupler[level]), inverse[level])
        for repeat in range(outer - 1):
            a = lax.ppermute(solved, "grp", cross)
            b = lax.ppermute(solved, "grp", straight)
            before = jnp.where(chip == 0, 0.0, jnp.where(first, a, b))
            z = jnp.where(first, before, u_other - product(product(before, coupler_p[level]), inverse_p[level]))
            solved = u_own - product(product(z, coupler[level]), inverse[level])
        results.append(solved)
        if level < levels - 1:
            contribution = jnp.dot(
                solved.astype(jnp.bfloat16), blocks[level], preferred_element_type=jnp.float32
            ).astype(jnp.bfloat16)
            ahead = routes[level] // rowblocks + level + 1
            target = routes[level] % rowblocks
            held = [] if held is None else held
            held.append((contribution, ahead, target))
            mine = to_chip == chip
            chunks = 0
            for value, value_level, value_row in held:
                hit = mine & (to_row == value_row) & (value_level == level + 1)
                chunks = chunks + jnp.where(hit[:, None, None], value[None].astype(jnp.float32), 0.0)
            received = lax.all_to_all(chunks.astype(jnp.bfloat16), axes, 0, 0, tiled=True)
            received = received.reshape(rowblocks * outer, INNER, nrhs, width)
            incoming[level + 1] = jnp.sum(received.astype(jnp.float32), axis=0)
    return jnp.stack(results, axis=0)[:, None, None]


def solution(mesh):
    return jax.shard_map(
        shards,
        mesh=mesh,
        in_specs=(
            P(None, "rows", "grp", None, None),
            P(None, "rows", "grp", None, None),
            P(None, "rows", "grp", None, None),
            P(None, "rows", "grp", None, None),
            P(None, "rows", "grp"),
        ),
        out_specs=P(None, "rows", "grp", None, None),
        check_vma=False,
    )
```

time: 80.9 us -> 61.4 us (0.76)
  starting transfers between devices: 36.1 us -> 12.6 us
  blocking collectives: 18.7 us -> 9.38 us
  waiting for transfers between devices: 5.4 us -> 10.6 us
  matrix products: 12.3 us -> 16.8 us
  other arithmetic: 1.01 us -> 2.95 us
  local copies, waits for them, and re-layouts: 1.39 us -> 2.23 us
    ppermute x9, starting transfers between devices: 36.1 us -> 7.56 us  [the longest x3 3.79 us: shards(): a = lax.ppermute(solved, 'grp', cross)]
    all_to_all x2 -> x1, blocking collectives: 18.7 us -> 9.38 us  [shards(): lax.all_to_all(chunks.astype(jnp.bfloat16), axes, 0, 0, tiled=True)]
    all_to_all x0 -> x1, starting transfers between devices: none -> 5.04 us  [shards(): lax.all_to_all(chunks.astype(jnp.bfloat16), axes, 0, 0, tiled=True)]
    all_to_all x0 -> x1, waiting for transfers between devices: none -> 4.48 us  [shards(): lax.all_to_all(chunks.astype(jnp.bfloat16), axes, 0, 0, tiled=True)]
    dot_general x23 -> x25, matrix products: 12.3 us -> 16.8 us  [the longest x23 15.4 us: product(): jnp.dot(jnp.concatenate([high, low], axis=0), w, preferred_element_type=j...]
    convert_element_type x0 -> x24, other arithmetic: none -> 2.03 us  [the longest x20 1.08 us: product(): low = (x - high.astype(jnp.float32)).astype(jnp.bfloat16)]
    slice x1 -> x2, local copies, waits for them, and re-layouts: 1.36 us -> 2.21 us  [the longest x1 1.39 us: shards(): target = routes[level] % rowblocks]
  transfers between devices with their start and end apart: 9 -> 10, of which waited for: 7 -> 7; matrix products, arithmetic and copies ran while one was open for 2% -> 9% of each run, Pallas kernels for 0% -> 0%
where the time goes in v1:
time: 61.4 us; the launch traced here: 60.2 us
  matrix products  16.8 us (27%)
  starting transfers between devices  12.6 us (21%)
  waiting for transfers between devices  10.6 us (17%)
  blocking collectives  9.38 us (15%)
  between operations  5.71 us (9%)
  other arithmetic  2.95 us (5%)
  local copies, waits for them, and re-layouts  2.23 us (4%)
    dot_general x23, matrix products, product(): jnp.dot(jnp.concatenate([high, low], axis=0), w, preferred_element_type=j...  15.4 us
    all_to_all x1, blocking collectives, shards(): lax.all_to_all(chunks.astype(jnp.bfloat16), axes, 0, 0, tiled=True)  9.38 us
    all_to_all x1, starting transfers between devices, shards(): lax.all_to_all(chunks.astype(jnp.bfloat16), axes, 0, 0, tiled=True)  5.04 us
    all_to_all x1, waiting for transfers between devices, shards(): lax.all_to_all(chunks.astype(jnp.bfloat16), axes, 0, 0, tiled=True)  4.48 us
    ppermute x3, waiting for transfers between devices, shards(): a = lax.ppermute(solved, 'grp', cross)  4.33 us
    ppermute x3, starting transfers between devices, shards(): a = lax.ppermute(solved, 'grp', cross)  3.79 us
    ppermute x3, starting transfers between devices, shards(): b = lax.ppermute(solved, 'grp', straight)  3.13 us
    ppermute x3, waiting for transfers between devices, shards(): b = lax.ppermute(solved, 'grp', straight)  1.79 us
  transfers between devices with their start and end apart: 10, of which 7 were waited for; matrix products, arithmetic and copies ran while one was open for 9% of the time, Pallas kernels for 0%

profile of v1, /device:TPU:1, one launch (start us, length us, event | category | flops | bytes accessed | tf_op | source)
XLA Modules:
  0.0 60.2 jit_solution(1972589214284473892)
XLA Ops:
  0.0 0.8 %fusion.143 = (bf16[2,512]{1,0:T(2,128)(2,1)S(1)}, bf16[2,512]{1,0:T(2,128)(2,1)S(1)}) fusion(f32[3,1,1,2,512]{4,3,2,1,0:T(2,128)} %param.5), kind=kLoop, calls=%fused_computation.188 | loop fusion | flops 3072 | bytes 10240 | tf_op jit(solution)/shard_map/convert_element_type | solution.py:11
  0.8 1.2 %fusion.36 = f32[4,512]{1,0:T(4,128)S(1)} fusion(bf16[3,1,1,512,512]{4,3,2,1,0:T(8,128)(2,1)} %param.6, bf16[2,512]{1,0:T(2,128)(2,1)S(1)} %get-tuple-element.48, bf16[2,512]{1,0:T(2,128)(2,1)S(1)} %get-tuple-element.49), kind=kOutput, calls=%fused_computation.44 | convolution fusion | flops 2105344 | bytes 536576 | tf_op jit(solution)/shard_map/dot_general | solution.py:12
  2.1 0.8 %slice_bitcast_fusion.14 = f32[2,2,512]{2,1,0:T(2,128)S(1)} fusion(f32[3,1,1,2,512]{4,3,0,2,1:T(2,128)} %bitcast.116), kind=kLoop, calls=%fused_computation.73 | loop fusion | bytes 16384 | tf_op jit(solution)/shard_map/slice | solution.py:33
  3.0 0.5 collective-permute-start.4
  3.5 1.4 %fusion.192 = (s32[1,1,1]{0,2,1:T(1,128)}, s32[1,1,1]{0,2,1:T(1,128)}) fusion(s32[2,1,1]{0,2,1:T(1,128)} %param.9), kind=kLoop, calls=%fused_computation.268 | loop fusion | bytes 16 | tf_op jit(solution)/shard_map/slice | solution.py:63
  7.6 1.2 %fusion.30 = f32[4,512]{1,0:T(4,128)S(1)} fusion(bf16[3,1,1,512,512]{4,3,2,1,0:T(8,128)(2,1)} %param.7, bf16[2,512]{1,0:T(2,128)(2,1)S(1)} %get-tuple-element.46, bf16[2,512]{1,0:T(2,128)(2,1)S(1)} %get-tuple-element.47), kind=kOutput, calls=%fused_computation.38 | convolution fusion | flops 2105344 | bytes 536576 | tf_op jit(solution)/shard_map/dot_general | solution.py:12
  8.8 1.2 %fusion.34 = f32[4,512]{1,0:T(4,128)S(1)} fusion(bf16[3,1,1,512,512]{4,3,2,1,0:T(8,128)(2,1)} %param.6, bf16[2,512]{1,0:T(2,128)(2,1)S(1)} %get-tuple-element.44, bf16[2,512]{1,0:T(2,128)(2,1)S(1)} %get-tuple-element.45), kind=kOutput, calls=%fused_computation.42 | convolution fusion | flops 2105344 | bytes 536576 | tf_op jit(solution)/shard_map/dot_general | solution.py:12
  10.1 2.7 %collective-permute-start.2 = (f32[2,512]{1,0:T(2,128)S(1)}, f32[2,512]{1,0:T(2,128)S(1)}, u32[]{:S(2)}, u32[]{:S(2)}) collective-permute-start(f32[2,512]{1,0:T(2,128)S(1)} %fusion.73), channel_id=1, source_target_pairs={{0,2},{1,3},{2,0},{3,1},{4,6},{5,7},{6,4},{7,5},{8,10},{9,11},{10,... | collective-permute-start | bytes 12296 | tf_op jit(solution)/shard_map/ppermute | solution.py:53
  12.8 0.9 %collective-permute-done.2 = f32[2,512]{1,0:T(2,128)S(1)} collective-permute-done((f32[2,512]{1,0:T(2,128)S(1)}, f32[2,512]{1,0:T(2,128)S(1)}, u32[]{:S(2)}, u32[]{:S(2)}) %collective-permute-start.2) | collective-permute-done | bytes 4128 | tf_op jit(solution)/shard_map/ppermute | solution.py:53
  13.7 2.0 %collective-permute-done.1 = f32[2,512]{1,0:T(2,128)S(1)} collective-permute-done((f32[2,512]{1,0:T(2,128)S(1)}, f32[2,512]{1,0:T(2,128)S(1)}, u32[]{:S(2)}, u32[]{:S(2)}) %collective-permute-start.1) | collective-permute-done | bytes 4128 | tf_op jit(solution)/shard_map/ppermute | solution.py:52
  15.8 1.2 %fusion.5 = f32[4,512]{1,0:T(4,128)S(1)} fusion(bf16[3,512,512]{2,1,0:T(8,128)(2,1)} %collective-permute-done.3, bf16[2,512]{1,0:T(2,128)(2,1)S(1)} %get-tuple-element.41, bf16[2,512]{1,0:T(2,128)(2,1)S(1)} %get-tuple-element.42), kind=kOutput, calls=%fused_computation.13 | convolution fusion | flops 2105344 | bytes 536576 | tf_op jit(solution)/shard_map/dot_general | solution.py:12
  17.1 1.2 %fusion.4 = f32[4,512]{1,0:T(4,128)S(1)} fusion(bf16[3,512,512]{2,1,0:T(8,128)(2,1)} %collective-permute-done.4, bf16[2,512]{1,0:T(2,128)(2,1)S(1)} %get-tuple-element.39, bf16[2,512]{1,0:T(2,128)(2,1)S(1)} %get-tuple-element.40), kind=kOutput, calls=%fused_computation.11 | convolution fusion | flops 2105344 | bytes 536576 | tf_op jit(solution)/shard_map/dot_general | solution.py:12
  18.7 1.2 %fusion.1 = f32[2,512]{1,0:T(2,128)S(1)} fusion(bf16[2,1,1,512,512]{4,3,2,1,0:T(8,128)(2,1)} %param.8, f32[2,512]{1,0:T(2,128)S(1)} %fusion.70), kind=kOutput, calls=%fused_computation.3 | convolution fusion | flops 1051648 | bytes 532480 | tf_op jit(solution)/shard_map/dot_general | solution.py:59
  19.9 0.8 %select_convert_fusion = bf16[32,2,512]{2,1,0:T(2,128)(2,1)} fusion(pred[32]{0:T(512)(128)(4,1)S(1)} %broadcast_and_fusion.1, f32[2,512]{1,0:T(2,128)S(1)} %fusion.1), kind=kLoop, calls=%fused_computation.70 | loop fusion | flops 32768 | bytes 69664 | tf_op jit(solution)/shard_map/convert_element_type | solution.py:71
  20.7 5.0 %all-to-all-start = ((bf16[32,2,512]{2,1,0:T(2,128)(2,1)}), bf16[32,2,512]{2,1,0:T(2,128)(2,1)S(1)}, u32[]{:S(2)}, u32[]{:S(2)}) async-start(bf16[32,2,512]{2,1,0:T(2,128)(2,1)} %select_convert_fusion), calls=%async_computation | async-start | bytes 131072 | tf_op jit(solution)/shard_map/all_to_all | solution.py:71
  28.5 4.5 %all-to-all-done = bf16[32,2,512]{2,1,0:T(2,128)(2,1)S(1)} async-done(((bf16[32,2,512]{2,1,0:T(2,128)(2,1)}), bf16[32,2,512]{2,1,0:T(2,128)(2,1)S(1)}, u32[]{:S(2)}, u32[]{:S(2)}) %all-to-all-start) | async-done | bytes 65568 | tf_op jit(solution)/shard_map/all_to_all | solution.py:71
  33.1 1.2 %fusion.41 = f32[4,512]{1,0:T(4,128)S(1)} fusion(bf16[3,512,512]{2,1,0:T(8,128)(2,1)} %collective-permute-done.4, bf16[2,512]{1,0:T(2,128)(2,1)S(1)} %get-tuple-element.33, bf16[2,512]{1,0:T(2,128)(2,1)S(1)} %get-tuple-element.34), kind=kOutput, calls=%fused_computation.49 | convolution fusion | flops 2105344 | bytes 536576 | tf_op jit(solution)/shard_map/dot_general | solution.py:12
  34.9 0.2 collective-permute-start.6
  35.1 1.9 %collective-permute-start.5 = (f32[2,512]{1,0:T(2,128)S(1)}, f32[2,512]{1,0:T(2,128)S(1)}, u32[]{:S(2)}, u32[]{:S(2)}) collective-permute-start(f32[2,512]{1,0:T(2,128)S(1)} %fusion.68), channel_id=1, source_target_pairs={{0,3},{1,2},{2,1},{3,0},{4,7},{5,6},{6,5},{7,4},{8,11},{9,10},{10,... | collective-permute-start | bytes 12296 | tf_op jit(solution)/shard_map/ppermute | solution.py:52
  37.0 0.4 collective-permute-done.6
  37.4 1.1 %collective-permute-done.5 = f32[2,512]{1,0:T(2,128)S(1)} collective-permute-done((f32[2,512]{1,0:T(2,128)S(1)}, f32[2,512]{1,0:T(2,128)S(1)}, u32[]{:S(2)}, u32[]{:S(2)}) %collective-permute-start.5) | collective-permute-done | bytes 4128 | tf_op jit(solution)/shard_map/ppermute | solution.py:52
  38.6 1.2 %fusion.3 = f32[4,512]{1,0:T(4,128)S(1)} fusion(bf16[3,512,512]{2,1,0:T(8,128)(2,1)} %collective-permute-done.3, bf16[2,512]{1,0:T(2,128)(2,1)S(1)} %get-tuple-element.26, bf16[2,512]{1,0:T(2,128)(2,1)S(1)} %get-tuple-element.27), kind=kOutput, calls=%fused_computation.8 | convolution fusion | flops 2105344 | bytes 536576 | tf_op jit(solution)/shard_map/dot_general | solution.py:12
  39.8 1.2 %fusion.40 = f32[4,512]{1,0:T(4,128)S(1)} fusion(bf16[3,512,512]{2,1,0:T(8,128)(2,1)} %collective-permute-done.4, bf16[2,512]{1,0:T(2,128)(2,1)S(1)} %get-tuple-element.24, bf16[2,512]{1,0:T(2,128)(2,1)S(1)} %get-tuple-element.25), kind=kOutput, calls=%fused_computation.48 | convolution fusion | flops 2105344 | bytes 536576 | tf_op jit(solution)/shard_map/dot_general | solution.py:12
  41.8 9.4 %all_to_all.10 = bf16[32,2,512]{2,1,0:T(2,128)(2,1)S(1)} all-to-all(bf16[32,2,512]{2,1,0:T(2,128)(2,1)S(1)} %add_convert_fusion), channel_id=1, replica_groups=mesh['rows'=8,'grp'=4] {'rows','grp'}, dimensions={0} | all-to-all | bytes 131072 | tf_op jit(solution)/shard_map/all_to_all | solution.py:71
  51.3 1.2 %fusion.43 = f32[4,512]{1,0:T(4,128)S(1)} fusion(bf16[3,512,512]{2,1,0:T(8,128)(2,1)} %collective-permute-done.4, bf16[2,512]{1,0:T(2,128)(2,1)S(1)} %get-tuple-element.18, bf16[2,512]{1,0:T(2,128)(2,1)S(1)} %get-tuple-element.19), kind=kOutput, calls=%fused_computation.51 | convolution fusion | flops 2105344 | bytes 536576 | tf_op jit(solution)/shard_map/dot_general | solution.py:12
  53.1 0.2 collective-permute-start.8
  53.3 1.9 %collective-permute-start.7 = (f32[2,512]{1,0:T(2,128)S(1)}, f32[2,512]{1,0:T(2,128)S(1)}, u32[]{:S(2)}, u32[]{:S(2)}) collective-permute-start(f32[2,512]{1,0:T(2,128)S(1)} %fusion.63), channel_id=1, source_target_pairs={{0,3},{1,2},{2,1},{3,0},{4,7},{5,6},{6,5},{7,4},{8,11},{9,10},{10,... | collective-permute-start | bytes 12296 | tf_op jit(solution)/shard_map/ppermute | solution.py:52
  55.2 0.4 collective-permute-done.8
  55.6 1.1 %collective-permute-done.7 = f32[2,512]{1,0:T(2,128)S(1)} collective-permute-done((f32[2,512]{1,0:T(2,128)S(1)}, f32[2,512]{1,0:T(2,128)S(1)}, u32[]{:S(2)}, u32[]{:S(2)}) %collective-permute-start.7) | collective-permute-done | bytes 4128 | tf_op jit(solution)/shard_map/ppermute | solution.py:52
  56.8 1.2 %fusion.2 = f32[4,512]{1,0:T(4,128)S(1)} fusion(bf16[3,512,512]{2,1,0:T(8,128)(2,1)} %collective-permute-done.3, bf16[2,512]{1,0:T(2,128)(2,1)S(1)} %get-tuple-element.11, bf16[2,512]{1,0:T(2,128)(2,1)S(1)} %get-tuple-element.12), kind=kOutput, calls=%fused_computation.5 | convolution fusion | flops 2105344 | bytes 536576 | tf_op jit(solution)/shard_map/dot_general | solution.py:12
  58.0 1.2 %fusion.42 = f32[4,512]{1,0:T(4,128)S(1)} fusion(bf16[3,512,512]{2,1,0:T(8,128)(2,1)} %collective-permute-done.4, bf16[2,512]{1,0:T(2,128)(2,1)S(1)} %get-tuple-element.9, bf16[2,512]{1,0:T(2,128)(2,1)S(1)} %get-tuple-element.10), kind=kOutput, calls=%fused_computation.50 | convolution fusion | flops 2105344 | bytes 536576 | tf_op jit(solution)/shard_map/dot_general | solution.py:12
  59.6 0.6 %maximum_bitcast_fusion = f32[3,1,1,2,512]{4,3,2,1,0:T(2,128)} fusion(f32[1,2,512]{2,1,0:T(2,128)S(1)} %fusion.60, f32[1,2,512]{2,1,0:T(2,128)S(1)} %bitcast.118, f32[1,2,512]{2,1,0:T(2,128)S(1)} %bitcast.117), kind=kLoop, calls=%fused_computation.72 | loop fusion | flops 6144 | bytes 24576 | tf_op jit(solution)/shard_map/broadcast_in_dim | solution.py:74
  (62 shorter events, 3.2 us)
Async XLA Ops:
  0.0 18.3 %copy-start.1 = (bf16[3,1,1,512,512]{4,3,2,1,0:T(8,128)(2,1)S(1)}, bf16[3,1,1,512,512]{4,3,2,1,0:T(8,128)(2,1)}, u32[]{:S(2)}) copy-start(bf16[3,1,1,512,512]{4,3,2,1,0:T(8,128)(2,1)} %param.7) | copy-start | bytes 4718596
  2.0 16.5 %copy-start = (bf16[3,1,1,512,512]{4,3,2,1,0:T(8,128)(2,1)S(1)}, bf16[3,1,1,512,512]{4,3,2,1,0:T(8,128)(2,1)}, u32[]{:S(2)}) copy-start(bf16[3,1,1,512,512]{4,3,2,1,0:T(8,128)(2,1)} %param.6) | copy-start | bytes 4718596
  2.9 4.7 %collective-permute-start = (f32[3,2,512]{2,1,0:T(2,128)S(1)}, f32[3,2,512]{2,1,0:T(2,128)S(1)}, u32[]{:S(2)}, u32[]{:S(2)}) collective-permute-start(f32[3,2,512]{2,1,0:T(2,128)S(1)} %pad_maximum_fusion), channel_id=1, source_target_pairs={{0,1},{1,0},{2,3},{3,2},{4,5},{5,4},{6,7},{7,6},{8,9},{9,8},{10,11... | collective-permute-start | bytes 36872 | tf_op jit(solution)/shard_map/ppermute | solution.py:33
  3.0 14.1 %collective-permute-start.4 = (bf16[3,512,512]{2,1,0:T(8,128)(2,1)}, bf16[3,512,512]{2,1,0:T(8,128)(2,1)}, u32[]{:S(2)}, u32[]{:S(2)}) collective-permute-start(bf16[3,512,512]{2,1,0:T(8,128)(2,1)} %bitcast.112), channel_id=1, source_target_pairs={{0,1},{1,0},{2,3},{3,2},{4,5},{5,4},{6,7},{7,6},{8,9},{9,8},{10,11... | collective-permute-start | bytes 4718600 | tf_op jit(solution)/shard_map/ppermute | solution.py:34
  3.5 12.3 %collective-permute-start.3 = (bf16[3,512,512]{2,1,0:T(8,128)(2,1)}, bf16[3,512,512]{2,1,0:T(8,128)(2,1)}, u32[]{:S(2)}, u32[]{:S(2)}) collective-permute-start(bf16[3,512,512]{2,1,0:T(8,128)(2,1)} %bitcast.113), channel_id=1, source_target_pairs={{0,1},{1,0},{2,3},{3,2},{4,5},{5,4},{6,7},{7,6},{8,9},{9,8},{10,11... | collective-permute-start | bytes 4718600 | tf_op jit(solution)/shard_map/ppermute | solution.py:35
  10.0 23.0 %copy-start.3 = (f32[3,1,1,2,512]{4,3,2,1,0:T(2,128)S(1)}, f32[3,1,1,2,512]{4,3,2,1,0:T(2,128)}, u32[]{:S(2)}) copy-start(f32[3,1,1,2,512]{4,3,2,1,0:T(2,128)} %param.5) | copy-start | bytes 36868
  10.1 3.7 %collective-permute-start.2 = (f32[2,512]{1,0:T(2,128)S(1)}, f32[2,512]{1,0:T(2,128)S(1)}, u32[]{:S(2)}, u32[]{:S(2)}) collective-permute-start(f32[2,512]{1,0:T(2,128)S(1)} %fusion.73), channel_id=1, source_target_pairs={{0,2},{1,3},{2,0},{3,1},{4,6},{5,7},{6,4},{7,5},{8,10},{9,11},{10,... | collective-permute-start | bytes 12296 | tf_op jit(solution)/shard_map/ppermute | solution.py:53
  12.8 3.0 %collective-permute-start.1 = (f32[2,512]{1,0:T(2,128)S(1)}, f32[2,512]{1,0:T(2,128)S(1)}, u32[]{:S(2)}, u32[]{:S(2)}) collective-permute-start(f32[2,512]{1,0:T(2,128)S(1)} %fusion.73), channel_id=1, source_target_pairs={{0,3},{1,2},{2,1},{3,0},{4,7},{5,6},{6,5},{7,4},{8,11},{9,10},{10,... | collective-permute-start | bytes 12296 | tf_op jit(solution)/shard_map/ppermute | solution.py:52
  20.7 12.3 %all-to-all-start = ((bf16[32,2,512]{2,1,0:T(2,128)(2,1)}), bf16[32,2,512]{2,1,0:T(2,128)(2,1)S(1)}, u32[]{:S(2)}, u32[]{:S(2)}) async-start(bf16[32,2,512]{2,1,0:T(2,128)(2,1)} %select_convert_fusion), calls=%async_computation | async-start | bytes 131072 | tf_op jit(solution)/shard_map/all_to_all | solution.py:71
  34.5 6.9 %copy-start.2 = (bf16[2,1,1,512,512]{4,3,2,1,0:T(8,128)(2,1)S(1)}, bf16[2,1,1,512,512]{4,3,2,1,0:T(8,128)(2,1)}, u32[]{:S(2)}) copy-start(bf16[2,1,1,512,512]{4,3,2,1,0:T(8,128)(2,1)} %param.8) | copy-start | bytes 3145732
  34.9 2.5 %collective-permute-start.6 = (f32[2,512]{1,0:T(2,128)S(1)}, f32[2,512]{1,0:T(2,128)S(1)}, u32[]{:S(2)}, u32[]{:S(2)}) collective-permute-start(f32[2,512]{1,0:T(2,128)S(1)} %fusion.68), channel_id=1, source_target_pairs={{0,2},{1,3},{2,0},{3,1},{4,6},{5,7},{6,4},{7,5},{8,10},{9,11},{10,... | collective-permute-start | bytes 12296 | tf_op jit(solution)/shard_map/ppermute | solution.py:53
  35.1 3.5 %collective-permute-start.5 = (f32[2,512]{1,0:T(2,128)S(1)}, f32[2,512]{1,0:T(2,128)S(1)}, u32[]{:S(2)}, u32[]{:S(2)}) collective-permute-start(f32[2,512]{1,0:T(2,128)S(1)} %fusion.68), channel_id=1, source_target_pairs={{0,3},{1,2},{2,1},{3,0},{4,7},{5,6},{6,5},{7,4},{8,11},{9,10},{10,... | collective-permute-start | bytes 12296 | tf_op jit(solution)/shard_map/ppermute | solution.py:52
  53.1 2.5 %collective-permute-start.8 = (f32[2,512]{1,0:T(2,128)S(1)}, f32[2,512]{1,0:T(2,128)S(1)}, u32[]{:S(2)}, u32[]{:S(2)}) collective-permute-start(f32[2,512]{1,0:T(2,128)S(1)} %fusion.63), channel_id=1, source_target_pairs={{0,2},{1,3},{2,0},{3,1},{4,6},{5,7},{6,4},{7,5},{8,10},{9,11},{10,... | collective-permute-start | bytes 12296 | tf_op jit(solution)/shard_map/ppermute | solution.py:53
  53.3 3.5 %collective-permute-start.7 = (f32[2,512]{1,0:T(2,128)S(1)}, f32[2,512]{1,0:T(2,128)S(1)}, u32[]{:S(2)}, u32[]{:S(2)}) collective-permute-start(f32[2,512]{1,0:T(2,128)S(1)} %fusion.63), channel_id=1, source_target_pairs={{0,3},{1,2},{2,1},{3,0},{4,7},{5,6},{6,5},{7,4},{8,11},{9,10},{10,... | collective-permute-start | bytes 12296 | tf_op jit(solution)/shard_map/ppermute | solution.py:52
